TPU v7x, 32 devices: a whole 2x2x4 slice. The times are simulated.
32 devices in a mesh: wide: 4 (over x, core), narrow: 8 (over z, y).
Axes of the slice: x: 2, y: 2, z: 4, core: 2. Of those that a mesh axis runs over, the one named last changes fastest.
Arguments:
- velocity: float32 [3, 1, 4096, 4096], P(None, None, ('wide', 'narrow')), may hold values from -6 to 6
- plane_wavenumber: float32 [1], replicated, may hold values from 2 to 1024
Outputs:
- projected: float32 [3, 1, 4096, 4096], P(None, None, ('wide', 'narrow'))
All inputs are finite; a program needn't handle non-finite values.
Results may differ from a plain program's by a relative error of at most 0.00007.
Values sent between devices are 32-bit elements; how exact they have to be, the bound alone decides.
No kernel may reach another device: no remote copies, remote signals or barrier semaphores. Data moves between devices by JAX's collectives and lax.ppermute only.
A program may use at most 128 MiB of HBM per device.

v0:
```python
import math
import jax
import jax.numpy as jnp
from jax import lax
from jax.sharding import PartitionSpec as P

radix_split = 64
highest = lax.Precision.HIGHEST


def angle_tables(row_size, col_size, period, direction):
    product = jnp.arange(row_size)[:, None] * jnp.arange(col_size)[None, :] % period
    angles = direction * 2.0 * math.pi * product.astype(jnp.float32) / period
    return (jnp.cos(angles), jnp.sin(angles))


def complex_product(pattern, left_real, left_imag, table_real, table_imag):
    out_real = jnp.einsum(pattern, left_real, table_real, precision=highest) - jnp.einsum(
        pattern, left_imag, table_imag, precision=highest
    )
    out_imag = jnp.einsum(pattern, left_real, table_imag, precision=highest) + jnp.einsum(
        pattern, left_imag, table_real, precision=highest
    )
    return (out_real, out_imag)


def transform(real_part, imag_part, direction):
    length = real_part.shape[-1]
    inner_size = length // radix_split
    leading = real_part.shape[:-1]
    grid_real = real_part.reshape(leading + (radix_split, inner_size))
    grid_imag = imag_part.reshape(leading + (radix_split, inner_size))
    outer_cos, outer_sin = angle_tables(radix_split, radix_split, radix_split, direction)
    section_real, section_imag = complex_product(
        "...ab,ak->...kb", grid_real, grid_imag, outer_cos, outer_sin
    )
    twist_cos, twist_sin = angle_tables(radix_split, inner_size, length, direction)
    turned_real = section_real * twist_cos - section_imag * twist_sin
    turned_imag = section_real * twist_sin + section_imag * twist_cos
    inner_cos, inner_sin = angle_tables(inner_size, inner_size, inner_size, direction)
    final_real, final_imag = complex_product(
        "...kb,bm->...mk", turned_real, turned_imag, inner_cos, inner_sin
    )
    return (final_real.reshape(leading + (length,)), final_imag.reshape(leading + (length,)))


def project(lines, wave_x, wave_z, kept_line):
    groups, per_device, length_y = lines.shape
    shaped = lines.reshape(3, 2, groups // 6, per_device, length_y)
    spec_real, spec_imag = transform(shaped[:, 0], shaped[:, 1], -1.0)
    index_y = jnp.arange(length_y)
    signed_y = jnp.where(index_y <= length_y // 2, index_y, index_y - length_y)
    kept_y = jnp.abs(signed_y) <= length_y // 3
    retained = (kept_line & kept_y[None, None, :]).astype(jnp.float32)
    wave_y = signed_y.astype(jnp.float32)[None, None, :]
    wave_square = wave_x * wave_x + wave_y * wave_y + wave_z * wave_z
    waves = (wave_x, wave_y, wave_z)
    div_real = wave_x * spec_real[0] + wave_y * spec_real[1] + wave_z * spec_real[2]
    div_imag = wave_x * spec_imag[0] + wave_y * spec_imag[1] + wave_z * spec_imag[2]
    proj_real = jnp.stack(
        [
            (spec_real[component] - waves[component] * div_real / wave_square) * retained
            for component in range(3)
        ]
    )
    proj_imag = jnp.stack(
        [
            (spec_imag[component] - waves[component] * div_imag / wave_square) * retained
            for component in range(3)
        ]
    )
    back_real, back_imag = transform(proj_real, proj_imag, 1.0)
    return jnp.stack([back_real / length_y, back_imag / length_y], axis=1).reshape(
        groups, per_device, length_y
    )


def first_send(spectrum, first_size):
    groups, rows, span = spectrum.shape
    return (
        spectrum.reshape(groups, rows, first_size, span // first_size)
        .transpose(2, 0, 1, 3)
        .reshape(first_size, 1, -1)
    )


def second_send(received, first_size, second_size, groups, rows, per_device):
    shaped = received.reshape(first_size, groups, rows, second_size, per_device)
    return shaped.transpose(3, 1, 4, 0, 2).reshape(second_size, 1, -1)


def arrange_lines(received, first_size, second_size, groups, rows, per_device):
    shaped = received.reshape(second_size, groups, per_device, first_size, rows)
    ordered = shaped.transpose(1, 2, 0, 3, 4)
    return ordered.reshape(groups, per_device, -1)


def first_return(solved, first_size, second_size, rows):
    groups, per_device, _ = solved.shape
    shaped = solved.reshape(groups, per_device, second_size, first_size, rows).transpose(
        2, 0, 1, 3, 4
    )
    return shaped.reshape(second_size, 1, -1)


def second_return(received, first_size, second_size, groups, rows, per_device):
    shaped = received.reshape(second_size, groups, per_device, first_size, rows)
    return shaped.transpose(3, 1, 4, 0, 2).reshape(first_size, 1, -1)


def arrange_rows(received, first_size, groups, rows):
    shaped = received.reshape(first_size, groups, rows, -1)
    return shaped.transpose(1, 2, 0, 3).reshape(groups, rows, -1)


def local(velocity, plane_wavenumber):
    components, plane_count, row_count, x_length = velocity.shape
    wide_size = lax.axis_size("wide")
    narrow_size = lax.axis_size("narrow")
    device_count = wide_size * narrow_size
    keep_x = x_length // 3 + 1
    spec_real, spec_imag = transform(velocity, jnp.zeros_like(velocity), -1.0)
    spec_real = spec_real[..., :keep_x]
    spec_imag = spec_imag[..., :keep_x]
    per_device = (keep_x + device_count - 1) // device_count
    line_span = per_device * device_count
    gap = ((0, 0), (0, 0), (0, 0), (0, 0), (0, line_span - keep_x))
    stacked = jnp.stack([spec_real, spec_imag], axis=1)
    spectrum = jnp.pad(stacked, gap).reshape(components * 2 * plane_count, row_count, line_span)
    groups = spectrum.shape[0]
    halfway = lax.all_to_all(
        first_send(spectrum, narrow_size), "narrow", split_axis=0, concat_axis=1, tiled=True
    )
    outgoing = second_send(halfway, narrow_size, wide_size, groups, row_count, per_device)
    arrived = lax.all_to_all(outgoing, "wide", split_axis=0, concat_axis=1, tiled=True)
    lines = arrange_lines(arrived, narrow_size, wide_size, groups, row_count, per_device)
    line_start = (
        lax.axis_index("narrow") * (per_device * wide_size) + lax.axis_index("wide") * per_device
    )
    indices = line_start + jnp.arange(per_device)
    wave_x = indices.astype(jnp.float32)[None, :, None]
    wave_z = plane_wavenumber[:, None, None]
    kept_line = (indices < keep_x)[None, :, None]
    solved = project(lines, wave_x, wave_z, kept_line)
    halfway = lax.all_to_all(
        first_return(solved, narrow_size, wide_size, row_count),
        "wide",
        split_axis=0,
        concat_axis=1,
        tiled=True,
    )
    outgoing = second_return(halfway, narrow_size, wide_size, groups, row_count, per_device)
    arrived = lax.all_to_all(outgoing, "narrow", split_axis=0, concat_axis=1, tiled=True)
    returned = arrange_rows(arrived, narrow_size, groups, row_count)
    columns = returned.reshape(components, 2, plane_count, row_count, line_span)[..., :keep_x]
    weights = jnp.where(jnp.arange(keep_x) == 0, 1.0, 2.0).astype(jnp.float32)
    widen = ((0, 0), (0, 0), (0, 0), (0, x_length - keep_x))
    back_real = jnp.pad(columns[:, 0] * weights, widen)
    back_imag = jnp.pad(columns[:, 1] * weights, widen)
    out_real, out_imag = transform(back_real, back_imag, 1.0)
    return out_real / x_length


def solution(mesh):
    placed = (P(None, None, ("wide", "narrow"), None), P())
    return jax.shard_map(
        local,
        mesh=mesh,
        in_specs=placed,
        out_specs=P(None, None, ("wide", "narrow"), None),
        check_vma=False,
    )
```

profile of v0, /device:TPU:0, one launch (start us, length us, event | category | flops | bytes accessed | tf_op | source)
XLA Modules:
  0.0 851.3 jit_solution(1181814289955283655)
XLA Ops:
  16.1 13.6 %fusion.28 = f32[64,3,128,64]{2,0,3,1:T(8,128)} fusion(f32[3,128,64,64]{1,3,2,0:T(8,128)} %bitcast.346), kind=kOutput, calls=%fused_computation.39 | convolution fusion | flops 1208016896 | bytes 12582912 | tf_op jit(solution)/shard_map/...ab,ak->...kb/dot_general | solution.py:21
  29.7 19.1 %fusion.5 = (f32[3,128,64,64]{1,2,3,0:T(8,128)}, f32[3,128,64,64]{1,2,3,0:T(8,128)S(1)}) fusion(f32[64,64]{0,1:T(8,128)S(1)} %get-tuple-element.25, f32[64,64]{0,1:T(8,128)S(1)} %get-tuple-element.26, f32[64,3,128,64]{2,0,3,1:T(8,128)} %fusion.28, f32[64,3,128,64]{2,0,3,1:T(8,128)} %fusion.52, f32[64,3,128,64]{2,0,3,1:T(8,128)} %fusion.54, ...), kind=kOutput, calls=%fused_computation.11 | convolution fusion | flops 1220599808 | bytes 37781504 | tf_op jit(solution)/shard_map/...ab,ak->...kb/dot_general | solution.py:18
  48.8 9.5 %fusion.22 = f32[64,3,128,64]{2,0,3,1:T(8,128)S(1)} fusion(f32[3,128,64,64]{1,2,3,0:T(8,128)S(1)} %get-tuple-element.12), kind=kOutput, calls=%fused_computation.33 | convolution fusion | flops 1208016896 | bytes 12582912 | tf_op jit(solution)/shard_map/...kb,bm->...mk/dot_general | solution.py:18
  58.3 9.6 %fusion.20 = f32[64,3,128,64]{2,0,3,1:T(8,128)S(1)} fusion(f32[3,128,64,64]{1,2,3,0:T(8,128)S(1)} %get-tuple-element.12), kind=kOutput, calls=%fused_computation.31 | convolution fusion | flops 1208016896 | bytes 12582912 | tf_op jit(solution)/shard_map/...kb,bm->...mk/dot_general | solution.py:21
  68.0 9.7 %subtract_bitcast_fusion = f32[3,1,128,64,64]{2,3,4,0,1:T(8,128)S(1)} fusion(f32[64,3,128,64]{2,0,3,1:T(8,128)S(1)} %fusion.22, f32[3,128,64,64]{1,2,3,0:T(8,128)S(1)} %bitcast.349), kind=kOutput, calls=%fused_computation.22 | convolution fusion | flops 1209589760 | bytes 18874368 | tf_op jit(solution)/shard_map/...kb,bm->...mk/dot_general | solution.py:18
  81.5 10.0 %add_bitcast_fusion = f32[3,1,128,64,64]{2,3,4,0,1:T(8,128)S(1)} fusion(f32[64,3,128,64]{2,0,3,1:T(8,128)S(1)} %fusion.20, f32[3,128,64,64]{1,2,3,0:T(8,128)S(1)} %bitcast.349), kind=kOutput, calls=%fused_computation.21 | convolution fusion | flops 1209589760 | bytes 18874368 | tf_op jit(solution)/shard_map/...kb,bm->...mk/dot_general | solution.py:21
  109.1 12.0 %reshape.976 = f32[8,1,132096]{2,1,0:T(1,128)} reshape(f32[8,6,128,172]{3,2,1,0:T(8,128)} %copy.65) | data formatting | bytes 8454144 | tf_op jit(solution)/shard_map/reshape | solution.py:83
  121.0 102.0 %all_to_all.16 = f32[8,1,132096]{2,1,0:T(1,128)} all-to-all(f32[8,1,132096]{2,1,0:T(1,128)} %reshape.976), channel_id=1, replica_groups=mesh['wide'=4,'narrow'=8] {'narrow'}, dimensions={0} | all-to-all | bytes 8454144 | tf_op jit(solution)/shard_map/all_to_all | solution.py:131
  223.0 13.4 %reduce = f32[8,132096]{1,0:T(8,128)} reduce(f32[8,1,132096]{2,1,0:T(1,128)} %all_to_all.16, f32[]{:T(128)} %constant.129), dimensions={1}, to_apply=%all_to_all.8.reduce_sub_computation | reduce | bytes 8454148 | tf_op jit(solution)/shard_map/all_to_all | solution.py:131
  236.4 26.8 %reshape.953 = f32[8,6,128,4,43]{4,3,2,1,0:T(4,128)} reshape(f32[8,132096]{1,0:T(8,128)} %reduce) | data formatting | bytes 8454144 | tf_op jit(solution)/shard_map/reshape | solution.py:88
  263.2 9.2 %copy.67 = f32[4,6,43,8,128]{4,3,2,1,0:T(8,128)} copy(f32[4,6,43,8,128]{2,0,4,1,3:T(4,128)} %bitcast.354) | data formatting | bytes 8454144 | tf_op jit(solution)/shard_map/transpose | solution.py:89
  279.0 47.0 %all-to-all-done.1 = f32[4,1,264192]{2,1,0:T(1,128)} async-done(((f32[4,1,264192]{2,1,0:T(1,128)}), f32[4,1,264192]{2,1,0:T(1,128)}, u32[]{:S(2)}, u32[]{:S(2)}) %all-to-all-start.1) | async-done | bytes 4227104 | tf_op jit(solution)/shard_map/all_to_all | solution.py:135
  336.7 9.3 %fusion.259 = (f32[3,1,1,43,4096]{4,1,0,3,2:T(1,128)}, f32[3,1,1,43,4096]{4,1,0,3,2:T(1,128)S(1)}) fusion(f32[3,2,1,43,4096]{4,1,0,3,2:T(2,128)} %reshape_reshape.13), kind=kLoop, calls=%fused_computation.298 | loop fusion | bytes 8454144 | tf_op jit(solution)/shard_map/slice | solution.py:50
  383.4 11.3 %fusion.42 = f32[64,3,43,64]{3,0,2,1:T(8,128)S(1)} fusion(f32[64,3,43,64]{3,0,2,1:T(8,128)S(1)} %convolution_add_fusion, f32[64,3,43,64]{3,0,2,1:T(8,128)S(1)} %convolution_subtract_fusion, f32[64,64]{1,0:T(8,128)S(1)} %copy.73, f32[64,64]{1,0:T(8,128)S(1)} %copy.72), kind=kOutput, calls=%fused_computation.60 | convolution fusion | flops 407441408 | bytes 6373376 | tf_op jit(solution)/shard_map/...kb,bm->...mk/dot_general | solution.py:21
  394.8 11.5 %fusion.44 = f32[64,3,43,64]{3,0,2,1:T(8,128)S(1)} fusion(f32[64,3,43,64]{3,0,2,1:T(8,128)S(1)} %convolution_add_fusion, f32[64,3,43,64]{3,0,2,1:T(8,128)S(1)} %convolution_subtract_fusion, f32[64,64]{1,0:T(8,128)S(1)} %copy.73, f32[64,64]{1,0:T(8,128)S(1)} %copy.72), kind=kOutput, calls=%fused_computation.62 | convolution fusion | flops 407441408 | bytes 6373376 | tf_op jit(solution)/shard_map/...kb,bm->...mk/dot_general | solution.py:18
  406.3 11.1 %add_bitcast_fusion.1 = f32[3,1,43,64,64]{4,3,2,0,1:T(8,128)S(1)} fusion(f32[64,3,43,64]{3,0,2,1:T(8,128)S(1)} %fusion.42, f32[64,3,43,64]{3,0,2,1:T(8,128)S(1)} %convolution_add_fusion, f32[64,3,43,64]{3,0,2,1:T(8,128)S(1)} %convolution_subtract_fusion, f32[64,64]{1,0:T(8,128)S(1)} %copy.73, f32[64,64]{1,0:T(8,128)S(1)} %copy.72), kind=kOutput, calls=%fused_computation.77 | convolution fusion | flops 407969792 | bytes 8486912 | tf_op jit(solution)/shard_map/...kb,bm->...mk/dot_general | solution.py:21
  417.4 11.3 %subtract_bitcast_fusion.1 = f32[3,1,43,64,64]{4,3,2,0,1:T(8,128)S(1)} fusion(f32[64,3,43,64]{3,0,2,1:T(8,128)S(1)} %fusion.44, f32[64,3,43,64]{3,0,2,1:T(8,128)S(1)} %convolution_add_fusion, f32[64,3,43,64]{3,0,2,1:T(8,128)S(1)} %convolution_subtract_fusion, f32[64,64]{1,0:T(8,128)S(1)} %copy.73, f32[64,64]{1,0:T(8,128)S(1)} %copy.72), kind=kOutput, calls=%fused_computation.78 | convolution fusion | flops 407969792 | bytes 8486912 | tf_op jit(solution)/shard_map/...kb,bm->...mk/dot_general | solution.py:18
  449.6 11.3 %fusion.34 = f32[64,3,43,64]{3,0,2,1:T(8,128)S(1)} fusion(f32[64,3,43,64]{3,0,2,1:T(8,128)S(1)} %fusion.67, f32[64,3,43,64]{3,0,2,1:T(8,128)S(1)} %fusion.66, f32[64,64]{1,0:T(8,128)S(1)} %copy.77, f32[64,64]{1,0:T(8,128)S(1)} %copy.76), kind=kOutput, calls=%fused_computation.48 | convolution fusion | flops 407441408 | bytes 6373376 | tf_op jit(solution)/shard_map/...kb,bm->...mk/dot_general | solution.py:18
  460.9 13.1 %fusion.32 = f32[64,3,43,64]{3,0,2,1:T(8,128)} fusion(f32[64,3,43,64]{3,0,2,1:T(8,128)S(1)} %fusion.67, f32[64,3,43,64]{3,0,2,1:T(8,128)S(1)} %fusion.66, f32[64,64]{1,0:T(8,128)S(1)} %copy.77, f32[64,64]{1,0:T(8,128)S(1)} %copy.76), kind=kOutput, calls=%fused_computation.46 | convolution fusion | flops 407441408 | bytes 6373376 | tf_op jit(solution)/shard_map/...kb,bm->...mk/dot_general | solution.py:21
  473.9 13.3 %multiply_bitcast_fusion.2 = f32[3,1,43,64,64]{4,3,2,0,1:T(8,128)} fusion(f32[64,3,43,64]{3,0,2,1:T(8,128)S(1)} %fusion.34, f32[64,3,43,64]{3,0,2,1:T(8,128)S(1)} %fusion.67, f32[64,3,43,64]{3,0,2,1:T(8,128)S(1)} %fusion.66, f32[64,64]{1,0:T(8,128)S(1)} %copy.77, f32[64,64]{1,0:T(8,128)S(1)} %copy.76), kind=kOutput, calls=%fused_computation.76 | convolution fusion | flops 408498176 | bytes 8486912 | tf_op jit(solution)/shard_map/...kb,bm->...mk/dot_general | solution.py:18
  492.3 17.7 %multiply_bitcast_fusion.1 = f32[3,1,43,64,64]{4,3,2,0,1:T(8,128)} fusion(f32[64,3,43,64]{3,0,2,1:T(8,128)} %fusion.32, f32[64,3,43,64]{3,0,2,1:T(8,128)} %copy-done.1, f32[64,3,43,64]{3,0,2,1:T(8,128)} %copy-done, f32[64,64]{1,0:T(8,128)S(1)} %copy.77, f32[64,64]{1,0:T(8,128)S(1)} %copy.76), kind=kOutput, calls=%fused_computation.75 | convolution fusion | flops 408498176 | bytes 8486912 | tf_op jit(solution)/shard_map/...kb,bm->...mk/dot_general | solution.py:21
  534.3 52.0 %all_to_all.17 = f32[4,1,264192]{2,1,0:T(1,128)} all-to-all(f32[4,1,264192]{2,1,0:T(1,128)S(1)} %bitcast.365), channel_id=1, replica_groups=mesh['wide'=4,'narrow'=8] {'wide'}, dimensions={0} | all-to-all | bytes 8454144 | tf_op jit(solution)/shard_map/all_to_all | solution.py:145
  595.3 20.3 %reshape.977 = f32[8,1,132096]{2,1,0:T(1,128)} reshape(f32[8,6,128,4,43]{4,3,2,1,0:T(4,128)} %bitcast.355) | data formatting | bytes 8454144 | tf_op jit(solution)/shard_map/reshape | solution.py:108
  620.4 94.2 %all-to-all-done.3 = f32[8,1,132096]{2,1,0:T(1,128)} async-done(((f32[8,1,132096]{2,1,0:T(1,128)}), f32[8,1,132096]{2,1,0:T(1,128)}, u32[]{:S(2)}, u32[]{:S(2)}) %all-to-all-start.3) | async-done | bytes 4227104 | tf_op jit(solution)/shard_map/all_to_all | solution.py:153
  714.6 13.2 %reduce.1 = f32[8,132096]{1,0:T(8,128)} reduce(f32[8,1,132096]{2,1,0:T(1,128)} %all-to-all-done.3, f32[]{:T(128)} %constant.129), dimensions={1}, to_apply=%all_to_all.11.reduce_sub_computation | reduce | bytes 8454148 | tf_op jit(solution)/shard_map/all_to_all | solution.py:153
  727.8 13.7 %reshape.967 = f32[8,6,128,172]{3,2,1,0:T(8,128)} reshape(f32[8,132096]{1,0:T(8,128)} %reduce.1) | data formatting | bytes 8454144 | tf_op jit(solution)/shard_map/reshape | solution.py:112
  755.3 13.5 %fusion.12 = f32[64,3,128,64]{2,0,3,1:T(8,128)} fusion(f32[3,128,64,64]{1,3,2,0:T(8,128)S(1)} %bitcast.352), kind=kOutput, calls=%fused_computation.23 | convolution fusion | flops 1208016896 | bytes 12582912 | tf_op jit(solution)/shard_map/...ab,ak->...kb/dot_general | solution.py:21
  768.8 13.0 %fusion.14 = f32[64,3,128,64]{2,0,3,1:T(8,128)} fusion(f32[3,128,64,64]{1,3,2,0:T(8,128)S(1)} %bitcast.353), kind=kOutput, calls=%fused_computation.25 | convolution fusion | flops 1208016896 | bytes 12582912 | tf_op jit(solution)/shard_map/...ab,ak->...kb/dot_general | solution.py:18
  782.1 13.2 %fusion.16 = f32[64,3,128,64]{2,0,3,1:T(8,128)} fusion(f32[3,128,64,64]{1,3,2,0:T(8,128)S(1)} %bitcast.350), kind=kOutput, calls=%fused_computation.27 | convolution fusion | flops 1208016896 | bytes 12582912 | tf_op jit(solution)/shard_map/...ab,ak->...kb/dot_general | solution.py:21
  795.3 19.8 %fusion.1 = (f32[3,128,64,64]{1,2,3,0:T(8,128)}, f32[3,128,64,64]{1,2,3,0:T(8,128)}) fusion(f32[64,64]{0,1:T(8,128)S(1)} %get-tuple-element.27, f32[64,64]{0,1:T(8,128)S(1)} %get-tuple-element.28, f32[64,3,128,64]{2,0,3,1:T(8,128)} %fusion.16, f32[64,3,128,64]{2,0,3,1:T(8,128)} %fusion.12, f32[64,3,128,64]{2,0,3,1:T(8,128)} %fusion.14, ...), kind=kOutput, calls=%fused_computation.3 | convolution fusion | flops 1220599808 | bytes 37781504 | tf_op jit(solution)/shard_map/...ab,ak->...kb/dot_general | solution.py:18
  815.2 12.6 %fusion.8 = f32[64,3,128,64]{2,0,3,1:T(8,128)S(1)} fusion(f32[3,128,64,64]{1,2,3,0:T(8,128)} %get-tuple-element.10), kind=kOutput, calls=%fused_computation.16 | convolution fusion | flops 1208016896 | bytes 12582912 | tf_op jit(solution)/shard_map/...kb,bm->...mk/dot_general | solution.py:18
  827.8 10.2 %multiply_bitcast_fusion = f32[3,1,128,64,64]{2,3,4,0,1:T(8,128)S(1)} fusion(f32[64,3,128,64]{2,0,3,1:T(8,128)S(1)} %fusion.8, f32[3,128,64,64]{1,2,3,0:T(8,128)S(1)} %bitcast.357), kind=kOutput, calls=%fused_computation.20 | convolution fusion | flops 1211162624 | bytes 18874368 | tf_op jit(solution)/shard_map/...kb,bm->...mk/dot_general | solution.py:18
  (85 shorter events, 182.1 us)
Async XLA Ops:
  48.8 19.2 %slice-start = ((s8[6291456]{0:T(1024)(128)(4,1)}), s8[4194304]{0:T(1024)(128)(4,1)S(1)}, s32[]{:S(2)}) async-start(s8[6291456]{0:T(1024)(128)(4,1)} %bitcast.348), calls=%async_computation.4 | async-start | bytes 8388608
  58.3 9.7 %slice-start.1 = ((s8[6291456]{0:T(1024)(128)(4,1)}), s8[2097152]{0:T(1024)(128)(4,1)S(1)}, s32[]{:S(2)}) async-start(s8[6291456]{0:T(1024)(128)(4,1)} %bitcast.348), calls=%async_computation.5 | async-start | bytes 4194304
  272.5 53.6 %all-to-all-start.1 = ((f32[4,1,264192]{2,1,0:T(1,128)}), f32[4,1,264192]{2,1,0:T(1,128)}, u32[]{:S(2)}, u32[]{:S(2)}) async-start(f32[4,1,264192]{2,1,0:T(1,128)} %bitcast.366), calls=%async_computation.1 | async-start | bytes 8454144 | tf_op jit(solution)/shard_map/all_to_all | solution.py:135
  351.5 8.2 copy-start.3
  359.7 6.0 copy-start.4
  367.4 11.6 %slice-start.4 = ((s8[4227072]{0:T(1024)(128)(4,1)}), s8[32768]{0:T(1024)(128)(4,1)S(1)}, s32[]{:S(2)}) async-start(s8[4227072]{0:T(1024)(128)(4,1)} %bitcast.361), calls=%async_computation.8 | async-start | bytes 65536
  371.0 8.0 copy-start.2
  371.0 8.0 slice-start.5
  445.1 28.9 %copy-start = (f32[64,3,43,64]{3,0,2,1:T(8,128)}, f32[64,3,43,64]{3,0,2,1:T(8,128)S(1)}, u32[]{:S(2)}) copy-start(f32[64,3,43,64]{3,0,2,1:T(8,128)S(1)} %fusion.66) | copy-start | bytes 6340612
  449.6 24.4 %copy-start.1 = (f32[64,3,43,64]{3,0,2,1:T(8,128)}, f32[64,3,43,64]{3,0,2,1:T(8,128)S(1)}, u32[]{:S(2)}) copy-start(f32[64,3,43,64]{3,0,2,1:T(8,128)S(1)} %fusion.67) | copy-start | bytes 6340612
  615.5 99.0 %all-to-all-start.3 = ((f32[8,1,132096]{2,1,0:T(1,128)}), f32[8,1,132096]{2,1,0:T(1,128)}, u32[]{:S(2)}, u32[]{:S(2)}) async-start(f32[8,1,132096]{2,1,0:T(1,128)} %reshape.977), calls=%async_computation.3 | async-start | bytes 8454144 | tf_op jit(solution)/shard_map/all_to_all | solution.py:153
  815.1 12.6 %slice-start.2 = ((s8[6291456]{0:T(1024)(128)(4,1)}), s8[4194304]{0:T(1024)(128)(4,1)S(1)}, s32[]{:S(2)}) async-start(s8[6291456]{0:T(1024)(128)(4,1)} %bitcast.356), calls=%async_computation.6 | async-start | bytes 8388608
  815.1 12.6 %slice-start.3 = ((s8[6291456]{0:T(1024)(128)(4,1)}), s8[2097152]{0:T(1024)(128)(4,1)S(1)}, s32[]{:S(2)}) async-start(s8[6291456]{0:T(1024)(128)(4,1)} %bitcast.356), calls=%async_computation.7 | async-start | bytes 4194304
where the time goes:
time: 859 us; the launch traced here: 851 us
  matrix products  308 us (36%)
  local copies, waits for them, and re-layouts  198 us (23%)
  blocking collectives  154 us (18%)
  waiting for transfers between devices  141 us (16%)
  other arithmetic  39 us (5%)
  starting transfers between devices  9.87 us (1%)
    all_to_all x1, blocking collectives, local(): lax.all_to_all(first_send(spectrum, narrow_size), 'narrow', split_axis=0,...  102 us
    dot_general x8, matrix products, complex_product(): jnp.einsum(pattern, left_real, table_real, precision=highest)  96.5 us
    all_to_all x1, waiting for transfers between devices, local(): lax.all_to_all(outgoing, 'narrow', split_axis=0, concat_axis=1, tiled=True)  94.2 us
    dot_general x7, matrix products, complex_product(): jnp.einsum(pattern, left_real, table_imag, precision=highest)  76.1 us
    dot_general x8, matrix products, complex_product(): jnp.einsum(pattern, left_imag, table_imag, precision=highest)  74.8 us
    dot_general x7, matrix products, complex_product(): jnp.einsum(pattern, left_imag, table_real, precision=highest)  60.6 us
    all_to_all x1, blocking collectives, local(): lax.all_to_all(first_return(solved, narrow_size, wide_size, row_count), '...  52 us
    all_to_all x1, waiting for transfers between devices, local(): lax.all_to_all(outgoing, 'wide', split_axis=0, concat_axis=1, tiled=True)  47 us
  transfers between devices with their start and end apart: 2, of which 2 were waited for; matrix products, arithmetic and copies ran while one was open for 0% of the time, Pallas kernels for 0%

commit v1 on v0

--- a/solution.py
+++ b/solution.py
@@ -132,7 +132,10 @@
         first_send(spectrum, narrow_size), "narrow", split_axis=0, concat_axis=1, tiled=True
     )
     outgoing = second_send(halfway, narrow_size, wide_size, groups, row_count, per_device)
-    arrived = lax.all_to_all(outgoing, "wide", split_axis=0, concat_axis=1, tiled=True)
+    arrived = jnp.concatenate(
+        lax.all_to_all(jnp.stack(jnp.split(outgoing, lax.axis_size("wide"), axis=0)), "wide", 0, 0),
+        axis=1,
+    )
     lines = arrange_lines(arrived, narrow_size, wide_size, groups, row_count, per_device)
     line_start = (
         lax.axis_index("narrow") * (per_device * wide_size) + lax.axis_index("wide") * per_device

time: 859 us -> 900 us (1.048)
  local copies, waits for them, and re-layouts: 198 us -> 231 us
    split x0 -> x5, local copies, waits for them, and re-layouts: none -> 42.1 us  [local(): jnp.split(outgoing, lax.axis_size('wide'), axis=0)]
    transpose x1 -> x0, local copies, waits for them, and re-layouts: 9.21 us -> none  [second_send(): return shaped.transpose(3, 1, 4, 0, 2).reshape(second_size, 1, -1)]
where the time goes in v1:
time: 900 us; the launch traced here: 892 us
  matrix products  308 us (34%)
  local copies, waits for them, and re-layouts  231 us (26%)
  blocking collectives  154 us (17%)
  waiting for transfers between devices  141 us (16%)
  other arithmetic  47.1 us (5%)
  starting transfers between devices  9.66 us (1%)
    all_to_all x1, blocking collectives, local(): lax.all_to_all(first_send(spectrum, narrow_size), 'narrow', split_axis=0,...  102 us
    dot_general x8, matrix products, complex_product(): jnp.einsum(pattern, left_real, table_real, precision=highest)  96.5 us
    all_to_all x1, waiting for transfers between devices, local(): lax.all_to_all(outgoing, 'narrow', split_axis=0, concat_axis=1, tiled=True)  94.2 us
    dot_general x7, matrix products, complex_product(): jnp.einsum(pattern, left_real, table_imag, precision=highest)  76.1 us
    dot_general x8, matrix products, complex_product(): jnp.einsum(pattern, left_imag, table_imag, precision=highest)  74.8 us
    dot_general x7, matrix products, complex_product(): jnp.einsum(pattern, left_imag, table_real, precision=highest)  60.6 us
    all_to_all x1, blocking collectives, local(): lax.all_to_all(first_return(solved, narrow_size, wide_size, row_count), '...  52 us
    all_to_all x1, waiting for transfers between devices, local(): lax.all_to_all(jnp.stack(jnp.split(outgoing, lax.axis_size('wide'), axis=...  47 us
  transfers between devices with their start and end apart: 2, of which 2 were waited for; matrix products, arithmetic and copies ran while one was open for 0% of the time, Pallas kernels for 0%

profile of v1, /device:TPU:0, one launch (start us, length us, event | category | flops | bytes accessed | tf_op | source)
XLA Modules:
  0.0 892.1 jit_solution(9983868670534154288)
XLA Ops:
  16.1 13.6 %fusion.28 = f32[64,3,128,64]{2,0,3,1:T(8,128)} fusion(f32[3,128,64,64]{1,3,2,0:T(8,128)} %bitcast.349), kind=kOutput, calls=%fused_computation.39 | convolution fusion | flops 1208016896 | bytes 12582912 | tf_op jit(solution)/shard_map/...ab,ak->...kb/dot_general | solution.py:21
  29.7 19.1 %fusion.5 = (f32[3,128,64,64]{1,2,3,0:T(8,128)}, f32[3,128,64,64]{1,2,3,0:T(8,128)S(1)}) fusion(f32[64,64]{0,1:T(8,128)S(1)} %get-tuple-element.29, f32[64,64]{0,1:T(8,128)S(1)} %get-tuple-element.30, f32[64,3,128,64]{2,0,3,1:T(8,128)} %fusion.28, f32[64,3,128,64]{2,0,3,1:T(8,128)} %fusion.52, f32[64,3,128,64]{2,0,3,1:T(8,128)} %fusion.54, ...), kind=kOutput, calls=%fused_computation.11 | convolution fusion | flops 1220599808 | bytes 37781504 | tf_op jit(solution)/shard_map/...ab,ak->...kb/dot_general | solution.py:18
  48.8 9.5 %fusion.22 = f32[64,3,128,64]{2,0,3,1:T(8,128)S(1)} fusion(f32[3,128,64,64]{1,2,3,0:T(8,128)S(1)} %get-tuple-element.12), kind=kOutput, calls=%fused_computation.33 | convolution fusion | flops 1208016896 | bytes 12582912 | tf_op jit(solution)/shard_map/...kb,bm->...mk/dot_general | solution.py:18
  58.3 9.6 %fusion.20 = f32[64,3,128,64]{2,0,3,1:T(8,128)S(1)} fusion(f32[3,128,64,64]{1,2,3,0:T(8,128)S(1)} %get-tuple-element.12), kind=kOutput, calls=%fused_computation.31 | convolution fusion | flops 1208016896 | bytes 12582912 | tf_op jit(solution)/shard_map/...kb,bm->...mk/dot_general | solution.py:21
  68.0 9.7 %subtract_bitcast_fusion = f32[3,1,128,64,64]{2,3,4,0,1:T(8,128)S(1)} fusion(f32[64,3,128,64]{2,0,3,1:T(8,128)S(1)} %fusion.22, f32[3,128,64,64]{1,2,3,0:T(8,128)S(1)} %bitcast.352), kind=kOutput, calls=%fused_computation.22 | convolution fusion | flops 1209589760 | bytes 18874368 | tf_op jit(solution)/shard_map/...kb,bm->...mk/dot_general | solution.py:18
  81.5 10.0 %add_bitcast_fusion = f32[3,1,128,64,64]{2,3,4,0,1:T(8,128)S(1)} fusion(f32[64,3,128,64]{2,0,3,1:T(8,128)S(1)} %fusion.20, f32[3,128,64,64]{1,2,3,0:T(8,128)S(1)} %bitcast.352), kind=kOutput, calls=%fused_computation.21 | convolution fusion | flops 1209589760 | bytes 18874368 | tf_op jit(solution)/shard_map/...kb,bm->...mk/dot_general | solution.py:21
  109.1 11.9 %reshape.973 = f32[8,1,132096]{2,1,0:T(1,128)} reshape(f32[8,6,128,172]{3,2,1,0:T(8,128)} %copy.68) | data formatting | bytes 8454144 | tf_op jit(solution)/shard_map/reshape | solution.py:83
  121.0 102.0 %all_to_all.32 = f32[8,1,132096]{2,1,0:T(1,128)} all-to-all(f32[8,1,132096]{2,1,0:T(1,128)} %reshape.973), channel_id=1, replica_groups=mesh['wide'=4,'narrow'=8] {'narrow'}, dimensions={0} | all-to-all | bytes 8454144 | tf_op jit(solution)/shard_map/all_to_all | solution.py:131
  223.0 13.4 %reduce = f32[8,132096]{1,0:T(8,128)} reduce(f32[8,1,132096]{2,1,0:T(1,128)} %all_to_all.32, f32[]{:T(128)} %constant.129), dimensions={1}, to_apply=%all_to_all.8.reduce_sub_computation | reduce | bytes 8454148 | tf_op jit(solution)/shard_map/all_to_all | solution.py:131
  236.4 26.8 %reshape.952 = f32[8,6,128,4,43]{4,3,2,1,0:T(4,128)} reshape(f32[8,132096]{1,0:T(8,128)} %reduce) | data formatting | bytes 8454144 | tf_op jit(solution)/shard_map/reshape | solution.py:88
  263.3 23.5 %fusion.259 = (f32[1,6,43,8,128]{2,0,4,1,3:T(1,128)}, f32[1,6,43,8,128]{2,0,4,1,3:T(1,128)S(1)}, f32[1,6,43,8,128]{2,0,4,1,3:T(1,128)}, f32[1,6,43,8,128]{2,0,4,1,3:T(1,128)}) fusion(f32[4,6,43,8,128]{2,0,4,1,3:T(4,128)} %bitcast.357), kind=kLoop, calls=%fused_computation.299 | loop fusion | bytes 8454144 | tf_op jit(solution)/shard_map/split | solution.py:136
  319.9 47.0 %all-to-all-done.1 = f32[4,1,1,264192]{3,2,1,0:T(1,128)} async-done(((f32[4,1,1,264192]{3,2,1,0:T(1,128)}), f32[4,1,1,264192]{3,2,1,0:T(1,128)}, u32[]{:S(2)}, u32[]{:S(2)}) %all-to-all-start.1) | async-done | bytes 4227104 | tf_op jit(solution)/shard_map/all_to_all | solution.py:136
  377.6 9.3 %fusion.260 = (f32[3,1,1,43,4096]{4,1,0,3,2:T(1,128)}, f32[3,1,1,43,4096]{4,1,0,3,2:T(1,128)S(1)}) fusion(f32[3,2,1,43,4096]{4,1,0,3,2:T(2,128)} %reshape_reshape.17), kind=kLoop, calls=%fused_computation.300 | loop fusion | bytes 8454144 | tf_op jit(solution)/shard_map/slice | solution.py:50
  424.3 11.3 %fusion.42 = f32[64,3,43,64]{3,0,2,1:T(8,128)S(1)} fusion(f32[64,3,43,64]{3,0,2,1:T(8,128)S(1)} %convolution_add_fusion, f32[64,3,43,64]{3,0,2,1:T(8,128)S(1)} %convolution_subtract_fusion, f32[64,64]{1,0:T(8,128)S(1)} %copy.78, f32[64,64]{1,0:T(8,128)S(1)} %copy.77), kind=kOutput, calls=%fused_computation.61 | convolution fusion | flops 407441408 | bytes 6373376 | tf_op jit(solution)/shard_map/...kb,bm->...mk/dot_general | solution.py:21
  435.6 11.5 %fusion.44 = f32[64,3,43,64]{3,0,2,1:T(8,128)S(1)} fusion(f32[64,3,43,64]{3,0,2,1:T(8,128)S(1)} %convolution_add_fusion, f32[64,3,43,64]{3,0,2,1:T(8,128)S(1)} %convolution_subtract_fusion, f32[64,64]{1,0:T(8,128)S(1)} %copy.78, f32[64,64]{1,0:T(8,128)S(1)} %copy.77), kind=kOutput, calls=%fused_computation.63 | convolution fusion | flops 407441408 | bytes 6373376 | tf_op jit(solution)/shard_map/...kb,bm->...mk/dot_general | solution.py:18
  447.1 11.1 %add_bitcast_fusion.1 = f32[3,1,43,64,64]{4,3,2,0,1:T(8,128)S(1)} fusion(f32[64,3,43,64]{3,0,2,1:T(8,128)S(1)} %fusion.42, f32[64,3,43,64]{3,0,2,1:T(8,128)S(1)} %convolution_add_fusion, f32[64,3,43,64]{3,0,2,1:T(8,128)S(1)} %convolution_subtract_fusion, f32[64,64]{1,0:T(8,128)S(1)} %copy.78, f32[64,64]{1,0:T(8,128)S(1)} %copy.77), kind=kOutput, calls=%fused_computation.78 | convolution fusion | flops 407969792 | bytes 8486912 | tf_op jit(solution)/shard_map/...kb,bm->...mk/dot_general | solution.py:21
  458.3 11.3 %subtract_bitcast_fusion.1 = f32[3,1,43,64,64]{4,3,2,0,1:T(8,128)S(1)} fusion(f32[64,3,43,64]{3,0,2,1:T(8,128)S(1)} %fusion.44, f32[64,3,43,64]{3,0,2,1:T(8,128)S(1)} %convolution_add_fusion, f32[64,3,43,64]{3,0,2,1:T(8,128)S(1)} %convolution_subtract_fusion, f32[64,64]{1,0:T(8,128)S(1)} %copy.78, f32[64,64]{1,0:T(8,128)S(1)} %copy.77), kind=kOutput, calls=%fused_computation.79 | convolution fusion | flops 407969792 | bytes 8486912 | tf_op jit(solution)/shard_map/...kb,bm->...mk/dot_general | solution.py:18
  490.4 11.3 %fusion.34 = f32[64,3,43,64]{3,0,2,1:T(8,128)S(1)} fusion(f32[64,3,43,64]{3,0,2,1:T(8,128)S(1)} %fusion.67, f32[64,3,43,64]{3,0,2,1:T(8,128)S(1)} %fusion.66, f32[64,64]{1,0:T(8,128)S(1)} %copy.82, f32[64,64]{1,0:T(8,128)S(1)} %copy.81), kind=kOutput, calls=%fused_computation.49 | convolution fusion | flops 407441408 | bytes 6373376 | tf_op jit(solution)/shard_map/...kb,bm->...mk/dot_general | solution.py:18
  501.7 13.1 %fusion.32 = f32[64,3,43,64]{3,0,2,1:T(8,128)} fusion(f32[64,3,43,64]{3,0,2,1:T(8,128)S(1)} %fusion.67, f32[64,3,43,64]{3,0,2,1:T(8,128)S(1)} %fusion.66, f32[64,64]{1,0:T(8,128)S(1)} %copy.82, f32[64,64]{1,0:T(8,128)S(1)} %copy.81), kind=kOutput, calls=%fused_computation.47 | convolution fusion | flops 407441408 | bytes 6373376 | tf_op jit(solution)/shard_map/...kb,bm->...mk/dot_general | solution.py:21
  514.8 13.3 %multiply_bitcast_fusion.2 = f32[3,1,43,64,64]{4,3,2,0,1:T(8,128)} fusion(f32[64,3,43,64]{3,0,2,1:T(8,128)S(1)} %fusion.34, f32[64,3,43,64]{3,0,2,1:T(8,128)S(1)} %fusion.67, f32[64,3,43,64]{3,0,2,1:T(8,128)S(1)} %fusion.66, f32[64,64]{1,0:T(8,128)S(1)} %copy.82, f32[64,64]{1,0:T(8,128)S(1)} %copy.81), kind=kOutput, calls=%fused_computation.77 | convolution fusion | flops 408498176 | bytes 8486912 | tf_op jit(solution)/shard_map/...kb,bm->...mk/dot_general | solution.py:18
  533.1 17.7 %multiply_bitcast_fusion.1 = f32[3,1,43,64,64]{4,3,2,0,1:T(8,128)} fusion(f32[64,3,43,64]{3,0,2,1:T(8,128)} %fusion.32, f32[64,3,43,64]{3,0,2,1:T(8,128)} %copy-done.1, f32[64,3,43,64]{3,0,2,1:T(8,128)} %copy-done, f32[64,64]{1,0:T(8,128)S(1)} %copy.82, f32[64,64]{1,0:T(8,128)S(1)} %copy.81), kind=kOutput, calls=%fused_computation.76 | convolution fusion | flops 408498176 | bytes 8486912 | tf_op jit(solution)/shard_map/...kb,bm->...mk/dot_general | solution.py:21
  575.2 52.0 %all_to_all.33 = f32[4,1,264192]{2,1,0:T(1,128)} all-to-all(f32[4,1,264192]{2,1,0:T(1,128)S(1)} %bitcast.368), channel_id=1, replica_groups=mesh['wide'=4,'narrow'=8] {'wide'}, dimensions={0} | all-to-all | bytes 8454144 | tf_op jit(solution)/shard_map/all_to_all | solution.py:148
  636.2 20.3 %reshape.974 = f32[8,1,132096]{2,1,0:T(1,128)} reshape(f32[8,6,128,4,43]{4,3,2,1,0:T(4,128)} %bitcast.358) | data formatting | bytes 8454144 | tf_op jit(solution)/shard_map/reshape | solution.py:108
  661.2 94.2 %all-to-all-done.3 = f32[8,1,132096]{2,1,0:T(1,128)} async-done(((f32[8,1,132096]{2,1,0:T(1,128)}), f32[8,1,132096]{2,1,0:T(1,128)}, u32[]{:S(2)}, u32[]{:S(2)}) %all-to-all-start.3) | async-done | bytes 4227104 | tf_op jit(solution)/shard_map/all_to_all | solution.py:156
  755.5 13.2 %reduce.1 = f32[8,132096]{1,0:T(8,128)} reduce(f32[8,1,132096]{2,1,0:T(1,128)} %all-to-all-done.3, f32[]{:T(128)} %constant.129), dimensions={1}, to_apply=%all_to_all.11.reduce_sub_computation | reduce | bytes 8454148 | tf_op jit(solution)/shard_map/all_to_all | solution.py:156
  768.7 13.7 %reshape.964 = f32[8,6,128,172]{3,2,1,0:T(8,128)} reshape(f32[8,132096]{1,0:T(8,128)} %reduce.1) | data formatting | bytes 8454144 | tf_op jit(solution)/shard_map/reshape | solution.py:112
  796.2 13.5 %fusion.12 = f32[64,3,128,64]{2,0,3,1:T(8,128)} fusion(f32[3,128,64,64]{1,3,2,0:T(8,128)S(1)} %bitcast.355), kind=kOutput, calls=%fused_computation.23 | convolution fusion | flops 1208016896 | bytes 12582912 | tf_op jit(solution)/shard_map/...ab,ak->...kb/dot_general | solution.py:21
  809.6 13.0 %fusion.14 = f32[64,3,128,64]{2,0,3,1:T(8,128)} fusion(f32[3,128,64,64]{1,3,2,0:T(8,128)S(1)} %bitcast.356), kind=kOutput, calls=%fused_computation.25 | convolution fusion | flops 1208016896 | bytes 12582912 | tf_op jit(solution)/shard_map/...ab,ak->...kb/dot_general | solution.py:18
  823.0 13.2 %fusion.16 = f32[64,3,128,64]{2,0,3,1:T(8,128)} fusion(f32[3,128,64,64]{1,3,2,0:T(8,128)S(1)} %bitcast.353), kind=kOutput, calls=%fused_computation.27 | convolution fusion | flops 1208016896 | bytes 12582912 | tf_op jit(solution)/shard_map/...ab,ak->...kb/dot_general | solution.py:21
  836.2 19.8 %fusion.1 = (f32[3,128,64,64]{1,2,3,0:T(8,128)}, f32[3,128,64,64]{1,2,3,0:T(8,128)}) fusion(f32[64,64]{0,1:T(8,128)S(1)} %get-tuple-element.31, f32[64,64]{0,1:T(8,128)S(1)} %get-tuple-element.32, f32[64,3,128,64]{2,0,3,1:T(8,128)} %fusion.16, f32[64,3,128,64]{2,0,3,1:T(8,128)} %fusion.12, f32[64,3,128,64]{2,0,3,1:T(8,128)} %fusion.14, ...), kind=kOutput, calls=%fused_computation.3 | convolution fusion | flops 1220599808 | bytes 37781504 | tf_op jit(solution)/shard_map/...ab,ak->...kb/dot_general | solution.py:18
  856.0 12.6 %fusion.8 = f32[64,3,128,64]{2,0,3,1:T(8,128)S(1)} fusion(f32[3,128,64,64]{1,2,3,0:T(8,128)} %get-tuple-element.10), kind=kOutput, calls=%fused_computation.16 | convolution fusion | flops 1208016896 | bytes 12582912 | tf_op jit(solution)/shard_map/...kb,bm->...mk/dot_general | solution.py:18
  868.7 10.2 %multiply_bitcast_fusion = f32[3,1,128,64,64]{2,3,4,0,1:T(8,128)S(1)} fusion(f32[64,3,128,64]{2,0,3,1:T(8,128)S(1)} %fusion.8, f32[3,128,64,64]{1,2,3,0:T(8,128)S(1)} %bitcast.360), kind=kOutput, calls=%fused_computation.20 | convolution fusion | flops 1211162624 | bytes 18874368 | tf_op jit(solution)/shard_map/...kb,bm->...mk/dot_general | solution.py:18
  (90 shorter events, 208.6 us)
Async XLA Ops:
  48.8 19.2 %slice-start = ((s8[6291456]{0:T(1024)(128)(4,1)}), s8[4194304]{0:T(1024)(128)(4,1)S(1)}, s32[]{:S(2)}) async-start(s8[6291456]{0:T(1024)(128)(4,1)} %bitcast.351), calls=%async_computation.4 | async-start | bytes 8388608
  58.3 9.7 %slice-start.1 = ((s8[6291456]{0:T(1024)(128)(4,1)}), s8[2097152]{0:T(1024)(128)(4,1)S(1)}, s32[]{:S(2)}) async-start(s8[6291456]{0:T(1024)(128)(4,1)} %bitcast.351), calls=%async_computation.5 | async-start | bytes 4194304
  313.5 53.4 %all-to-all-start.1 = ((f32[4,1,1,264192]{3,2,1,0:T(1,128)}), f32[4,1,1,264192]{3,2,1,0:T(1,128)}, u32[]{:S(2)}, u32[]{:S(2)}) async-start(f32[4,1,1,264192]{3,2,1,0:T(1,128)} %pad_maximum_fusion), calls=%async_computation.1 | async-start | bytes 8454144 | tf_op jit(solution)/shard_map/all_to_all | solution.py:136
  392.3 8.2 copy-start.3
  400.5 6.0 copy-start.4
  408.2 11.6 %slice-start.4 = ((s8[4227072]{0:T(1024)(128)(4,1)}), s8[32768]{0:T(1024)(128)(4,1)S(1)}, s32[]{:S(2)}) async-start(s8[4227072]{0:T(1024)(128)(4,1)} %bitcast.364), calls=%async_computation.8 | async-start | bytes 65536
  411.9 8.0 copy-start.2
  411.9 8.0 slice-start.5
  485.9 28.9 %copy-start = (f32[64,3,43,64]{3,0,2,1:T(8,128)}, f32[64,3,43,64]{3,0,2,1:T(8,128)S(1)}, u32[]{:S(2)}) copy-start(f32[64,3,43,64]{3,0,2,1:T(8,128)S(1)} %fusion.66) | copy-start | bytes 6340612
  490.4 24.4 %copy-start.1 = (f32[64,3,43,64]{3,0,2,1:T(8,128)}, f32[64,3,43,64]{3,0,2,1:T(8,128)S(1)}, u32[]{:S(2)}) copy-start(f32[64,3,43,64]{3,0,2,1:T(8,128)S(1)} %fusion.67) | copy-start | bytes 6340612
  656.4 99.0 %all-to-all-start.3 = ((f32[8,1,132096]{2,1,0:T(1,128)}), f32[8,1,132096]{2,1,0:T(1,128)}, u32[]{:S(2)}, u32[]{:S(2)}) async-start(f32[8,1,132096]{2,1,0:T(1,128)} %reshape.974), calls=%async_computation.3 | async-start | bytes 8454144 | tf_op jit(solution)/shard_map/all_to_all | solution.py:156
  856.0 12.6 %slice-start.2 = ((s8[6291456]{0:T(1024)(128)(4,1)}), s8[4194304]{0:T(1024)(128)(4,1)S(1)}, s32[]{:S(2)}) async-start(s8[6291456]{0:T(1024)(128)(4,1)} %bitcast.359), calls=%async_computation.6 | async-start | bytes 8388608
  856.0 12.6 %slice-start.3 = ((s8[6291456]{0:T(1024)(128)(4,1)}), s8[2097152]{0:T(1024)(128)(4,1)S(1)}, s32[]{:S(2)}) async-start(s8[6291456]{0:T(1024)(128)(4,1)} %bitcast.359), calls=%async_computation.7 | async-start | bytes 4194304
